TPU v7x, 32 devices: a whole 2x2x4 slice. The times are simulated.
32 devices in a mesh: gx: 2 (over x), gy: 4 (over y, core), gz: 4 (over z).
Axes of the slice: x: 2, y: 2, z: 4, core: 2. Of those that a mesh axis runs over, the one named last changes fastest.
Arguments:
- right_side: float32 [4, 5, 2, 32, 512], P(None, None, 'gx', 'gy', 'gz'), may hold values from -6 to 6
- jacobian: bfloat16 [27, 5, 5, 2, 32, 512], P(None, None, None, 'gx', 'gy', 'gz'), may hold values from -0.14 to 12.14, as said below
Outputs:
- solution: float32 [4, 5, 2, 32, 512], P(None, None, 'gx', 'gy', 'gz')
- residual: float32 [4, 5, 2, 32, 512], P(None, None, 'gx', 'gy', 'gz')
Inputs may be any that keep to these rules, and one draw needn't show every extreme that they name: `jacobian`: blocks of offsets other than 13 and the off-diagonal entries of block 13 lie within -0.14 to 0.14; the diagonal entries of block 13 exceed 5.8 in every cell.
All inputs are finite; a program needn't handle non-finite values.
Results may differ from a plain program's by a relative error of at most 0.0003.
Values sent between devices are 32-bit elements.
A program may use at most 64 MiB of HBM per device.

v0:
```python
import jax
import jax.numpy as jnp
from jax import lax
from jax.sharding import PartitionSpec as P

ITERS = 3


def extended(cells, sides, width):
    for axis, dim in sides:
        count = lax.axis_size(axis)
        head = lax.slice_in_dim(cells, 0, width, axis=dim)
        tail = lax.slice_in_dim(cells, cells.shape[dim] - width, cells.shape[dim], axis=dim)
        cells = jnp.concatenate(
            [
                lax.ppermute(tail, axis, [(i, (i + 1) % count) for i in range(count)]),
                cells,
                lax.ppermute(head, axis, [((i + 1) % count, i) for i in range(count)]),
            ],
            axis=dim,
        )
    return cells


def dot_high(left, right):
    return jnp.dot(left, right, precision=lax.Precision.HIGHEST, preferred_element_type=jnp.float32)


def lower_solve(factor, target):
    solved = []
    for row_pos in range(factor.shape[0]):
        accum = target[row_pos]
        for prior in range(row_pos):
            accum = accum - factor[row_pos, prior] * solved[prior]
        solved.append(accum / factor[row_pos, row_pos])
    return jnp.stack(solved)


def upper_solve(factor, target):
    size_all = factor.shape[0]
    solved = [None] * size_all
    for row_pos in range(size_all - 1, -1, -1):
        accum = target[row_pos]
        for later in range(row_pos + 1, size_all):
            accum = accum - factor[later, row_pos] * solved[later]
        solved[row_pos] = accum / factor[row_pos, row_pos]
    return jnp.stack(solved)


def extend(field):
    padded = extended(field, (("gx", 2), ("gy", 3), ("gz", 4)), 1)
    position = lax.axis_index("gz")
    bottom = jnp.where(position == 0, 0.0, 1.0).astype(jnp.float32)
    topmost = jnp.where(position == lax.axis_size("gz") - 1, 0.0, 1.0).astype(jnp.float32)
    inside = jnp.ones((padded.shape[4] - 2,), jnp.float32)
    scaling = jnp.concatenate([bottom[None], inside, topmost[None]])
    return padded * scaling


def apply_operator(jacobian, padded):
    extent_x = padded.shape[2] - 2
    extent_y = padded.shape[3] - 2
    extent_z = padded.shape[4] - 2
    total = jnp.zeros((padded.shape[0], padded.shape[1], extent_x, extent_y, extent_z), jnp.float32)
    for stencil_pos in range(27):
        start_x = stencil_pos // 9
        start_y = stencil_pos // 3 % 3
        start_z = stencil_pos % 3
        piece = padded[
            :,
            :,
            start_x : start_x + extent_x,
            start_y : start_y + extent_y,
            start_z : start_z + extent_z,
        ]
        block = jacobian[stencil_pos].astype(jnp.float32)
        for source_comp in range(block.shape[1]):
            total = total + block[None, :, source_comp] * piece[:, source_comp][:, None]
    return total


def shards(right_side, jacobian):
    field_shape = right_side.shape
    rhs_count = field_shape[0]
    flat_rhs = right_side.reshape(rhs_count, -1)
    start_matrix = lax.psum(dot_high(flat_rhs, flat_rhs.T), ("gx", "gy", "gz"))
    start_factor = jnp.linalg.cholesky(start_matrix)
    basis = [lower_solve(start_factor, flat_rhs)]
    hessen_rows = []
    products = []
    for iteration in range(ITERS):
        workspace = apply_operator(jacobian, extend(basis[-1].reshape(field_shape))).reshape(
            rhs_count, -1
        )
        products.append(workspace)
        stacked = jnp.concatenate(basis, axis=0)
        coefficients, raw_gram = lax.psum(
            (dot_high(stacked, workspace.T), dot_high(workspace, workspace.T)), ("gx", "gy", "gz")
        )
        workspace = workspace - dot_high(coefficients.T, stacked)
        gram_matrix = raw_gram - dot_high(coefficients.T, coefficients)
        factor = jnp.linalg.cholesky(gram_matrix)
        basis.append(lower_solve(factor, workspace))
        filler = jnp.zeros((rhs_count, rhs_count * (ITERS - iteration - 1)), jnp.float32)
        hessen_rows.append(jnp.concatenate([coefficients.T, factor, filler], axis=1))
    hessen = jnp.concatenate(hessen_rows, axis=0)
    target = jnp.concatenate(
        [start_factor, jnp.zeros((rhs_count, rhs_count * ITERS), jnp.float32)], axis=1
    )
    normal_factor = jnp.linalg.cholesky(dot_high(hessen, hessen.T))
    middle = lower_solve(normal_factor, dot_high(hessen, target.T))
    weights = upper_solve(normal_factor, middle)
    solution = dot_high(weights.T, jnp.concatenate(basis[:-1], axis=0))
    solution_field = solution.reshape(field_shape)
    residual = right_side - apply_operator(jacobian, extend(solution_field))
    return (solution_field, residual)


def solution(mesh):
    in_specs = (P(None, None, "gx", "gy", "gz"), P(None, None, None, "gx", "gy", "gz"))
    out_specs = (P(None, None, "gx", "gy", "gz"), P(None, None, "gx", "gy", "gz"))
    return jax.shard_map(shards, mesh=mesh, in_specs=in_specs, out_specs=out_specs, check_vma=False)
```

profile of v0, /device:TPU:0, one launch (start us, length us, event | category | flops | bytes accessed | tf_op | source)
XLA Modules:
  0.0 496.2 jit_solution(8846187615325379422)
XLA Ops:
  0.6 1.5 convolution_bitcast_fusion.4
  2.1 41.9 %psum.49 = f32[4,4]{0,1:T(4,128)S(1)} all-reduce(f32[4,4]{0,1:T(4,128)S(1)} %convolution_bitcast_fusion.4), channel_id=1, replica_groups=mesh['gx'=2,'gy'=4,'gz'=4] {'gx','gy','gz'}, use_global_device_ids=true, to_apply=%region_0.0 | all-reduce | flops 16 | bytes 128 | tf_op jit(solution)/shard_map/psum | solution.py:86
  46.6 4.5 subtract_divide_fusion.1
  51.0 5.3 %subtract_divide_fusion = (f32[1,5,1,8,128]{4,3,2,1,0:T(8,128)S(1)}, f32[1,5,1,8,128]{4,3,2,1,0:T(8,128)S(1)}, f32[1,5,1,8,128]{4,3,2,1,0:T(8,128)S(1)}, f32[1,5,1,8,128]{4,3,2,1,0:T(8,128)S(1)}) fusion(f32[1,5,1,8,128]{4,3,2,1,0:T(8,128)S(1)} %get-tuple-element.39, f32[1,5,1,8,128]{4,3,2,1,0:T(8,128)S(1)} %get-tuple-element.40, f32[]{:T(128)} %bitcast.16, ...), kind=kLoop, calls=%fused_computation.244 | loop fusion | flops 61440 | bytes 184348 | tf_op jit(solution)/shard_map/div | solution.py:35
  56.3 2.3 collective-permute-start.1
  60.2 5.8 %subtract_divide_fusion.3 = (f32[1,5120]{1,0:T(1,128)S(1)}, f32[1,5120]{1,0:T(1,128)S(1)}, f32[1,5120]{1,0:T(1,128)S(1)}) fusion(f32[1,5120]{1,0:T(1,128)S(1)} %bitcast.1697, f32[1,5120]{1,0:T(1,128)S(1)} %bitcast.1646, f32[]{:T(128)} %bitcast.16, f32[]{:T(128)} %bitcast.15, f32[]{:T(128)} %bitcast.14, f32[]{:T(128)} %bitcast.13, f32[]{:T(128)} %bitcast.11, ...), kind=kLoop, calls=%fused_computation.248 | loop fusion | flops 76800 | bytes 143396 | tf_op jit(solution)/shard_map/div | solution.py:35
  67.8 2.2 collective-permute-done.2
  70.3 2.2 collective-permute-start.5
  72.6 11.6 %collective-permute-done.5 = f32[4,5,3,10,1]{4,3,2,1,0:T(8,128)S(1)} collective-permute-done((f32[4,5,3,10,1]{4,3,2,1,0:T(8,128)S(1)}, f32[4,5,3,10,1]{4,3,2,1,0:T(8,128)S(1)}, u32[]{:S(2)}, u32[]{:S(2)}) %collective-permute-start.5) | collective-permute-done | bytes 2432 | tf_op jit(solution)/shard_map/ppermute | solution.py:18
  84.2 11.7 %collective-permute-done.4 = f32[4,5,3,10,1]{4,3,2,1,0:T(8,128)S(1)} collective-permute-done((f32[4,5,3,10,1]{4,3,2,1,0:T(8,128)S(1)}, f32[4,5,3,10,1]{4,3,2,1,0:T(8,128)S(1)}, u32[]{:S(2)}, u32[]{:S(2)}) %collective-permute-start.4) | collective-permute-done | bytes 2432 | tf_op jit(solution)/shard_map/ppermute | solution.py:16
  97.6 2.0 multiply_add_fusion.5
  100.5 38.5 %all-reduce.3 = (f32[4,4]{1,0:T(4,128)S(1)}, f32[4,4]{0,1:T(4,128)S(1)}) all-reduce(f32[4,4]{1,0:T(4,128)S(1)} %fusion.5, f32[4,4]{0,1:T(4,128)S(1)} %convolution_bitcast_fusion.3), channel_id=1, replica_groups=mesh['gx'=2,'gy'=4,'gz'=4] {'gx','gy','gz'}, use_global_device_ids=true, to_apply=%region_3.5 | all-reduce | flops 32 | bytes 256 | tf_op jit(solution)/shard_map/psum | solution.py:97
  142.0 6.5 %fusion.23 = (f32[1,5120]{1,0:T(1,128)S(1)}, f32[1,5120]{1,0:T(1,128)S(1)}, f32[1,5120]{1,0:T(1,128)S(1)}, f32[1,5120]{1,0:T(1,128)S(1)}) fusion(f32[4,5120]{1,0:T(4,128)S(1)} %convolution_subtract_fusion.1, f32[]{:T(128)} %bitcast.355, f32[]{:T(128)} %bitcast.354, f32[]{:T(128)} %bitcast.353, f32[]{:T(128)} %bitcast.352, f32[]{:T(128)} %bitcast.351, ...), kind=kLoop, calls=%fused_computation.254 | loop fusion | flops 81920 | bytes 163880 | tf_op jit(solution)/shard_map/div | solution.py:35
  148.5 2.3 collective-permute-start.7
  150.9 2.3 collective-permute-done.7
  153.3 2.0 collective-permute-done.6
  157.0 1.8 collective-permute-done.8
  158.8 1.1 fusion.42
  160.0 1.9 collective-permute-start.11
  162.2 11.6 %collective-permute-done.11 = f32[4,5,3,10,1]{4,3,2,1,0:T(8,128)} collective-permute-done((f32[4,5,3,10,1]{4,3,2,1,0:T(8,128)}, f32[4,5,3,10,1]{4,3,2,1,0:T(8,128)}, u32[]{:S(2)}, u32[]{:S(2)}) %collective-permute-start.11) | collective-permute-done | bytes 2432 | tf_op jit(solution)/shard_map/ppermute | solution.py:18
  173.8 10.6 %collective-permute-done.10 = f32[4,5,3,10,1]{4,3,2,1,0:T(8,128)} collective-permute-done((f32[4,5,3,10,1]{4,3,2,1,0:T(8,128)}, f32[4,5,3,10,1]{4,3,2,1,0:T(8,128)}, u32[]{:S(2)}, u32[]{:S(2)}) %collective-permute-start.10) | collective-permute-done | bytes 2432 | tf_op jit(solution)/shard_map/ppermute | solution.py:16
  184.4 1.9 maximum_multiply_fusion.1
  187.3 2.0 multiply_add_fusion.3
  190.2 38.3 %all-reduce.2 = (f32[8,4]{0,1:T(4,128)S(1)}, f32[4,4]{0,1:T(4,128)S(1)}) all-reduce(f32[8,4]{0,1:T(4,128)S(1)} %fusion.3, f32[4,4]{0,1:T(4,128)S(1)} %convolution_bitcast_fusion.2), channel_id=1, replica_groups=mesh['gx'=2,'gy'=4,'gz'=4] {'gx','gy','gz'}, use_global_device_ids=true, to_apply=%region_5.7 | all-reduce | flops 48 | bytes 384 | tf_op jit(solution)/shard_map/psum | solution.py:97
  231.4 6.5 %fusion.24 = (f32[1,5120]{1,0:T(1,128)S(1)}, f32[1,5120]{1,0:T(1,128)S(1)}, f32[1,5120]{1,0:T(1,128)S(1)}, f32[1,5120]{1,0:T(1,128)S(1)}) fusion(f32[4,5120]{1,0:T(4,128)S(1)} %convolution_subtract_fusion, f32[]{:T(128)} %bitcast.511, f32[]{:T(128)} %bitcast.510, f32[]{:T(128)} %bitcast.509, f32[]{:T(128)} %bitcast.508, f32[]{:T(128)} %bitcast.507, ...), kind=kLoop, calls=%fused_computation.255 | loop fusion | flops 81920 | bytes 163880 | tf_op jit(solution)/shard_map/div | solution.py:35
  237.9 2.3 collective-permute-start.13
  240.4 2.7 collective-permute-done.13
  243.1 1.7 collective-permute-done.12
  246.4 1.8 collective-permute-done.14
  249.4 2.3 collective-permute-start.17
  252.1 11.5 %collective-permute-done.17 = f32[4,5,3,10,1]{4,3,2,1,0:T(8,128)} collective-permute-done((f32[4,5,3,10,1]{4,3,2,1,0:T(8,128)}, f32[4,5,3,10,1]{4,3,2,1,0:T(8,128)}, u32[]{:S(2)}, u32[]{:S(2)}) %collective-permute-start.17) | collective-permute-done | bytes 2432 | tf_op jit(solution)/shard_map/ppermute | solution.py:18
  263.6 10.3 %collective-permute-done.16 = f32[4,5,3,10,1]{4,3,2,1,0:T(8,128)} collective-permute-done((f32[4,5,3,10,1]{4,3,2,1,0:T(8,128)}, f32[4,5,3,10,1]{4,3,2,1,0:T(8,128)}, u32[]{:S(2)}, u32[]{:S(2)}) %collective-permute-start.16) | collective-permute-done | bytes 2432 | tf_op jit(solution)/shard_map/ppermute | solution.py:16
  273.9 1.9 maximum_multiply_fusion.2
  276.8 2.1 multiply_add_fusion.1
  279.9 39.1 %all-reduce.1 = (f32[4,4]{0,1:T(4,128)S(1)}, f32[12,4]{0,1:T(4,128)S(1)}) all-reduce(f32[4,4]{0,1:T(4,128)S(1)} %convolution_bitcast_fusion.1, f32[12,4]{0,1:T(4,128)S(1)} %fusion), channel_id=1, replica_groups=mesh['gx'=2,'gy'=4,'gz'=4] {'gx','gy','gz'}, use_global_device_ids=true, to_apply=%region_8.10 | all-reduce | flops 64 | bytes 512 | tf_op jit(solution)/shard_map/psum | solution.py:97
  328.8 41.0 %subtract_divide_fusion.18 = (f32[1,4]{0,1:T(4,128)S(1)}, f32[1,4]{0,1:T(4,128)S(1)}, f32[1,4]{0,1:T(4,128)S(1)}, f32[1,4]{0,1:T(4,128)S(1)}, f32[1,4]{0,1:T(4,1...) fusion(f32[12,4]{0,1:T(4,128)S(1)} %fusion.30, ...), kind=kLoop, calls=%fused_computation.833 | loop fusion | flops 484 | bytes 600 | tf_op jit(solution)/shard_map/div | solution.py:35
  369.8 30.0 %subtract_divide_fusion.9 = (f32[1,4]{0,1:T(4,128)S(1)}, f32[1,4]{0,1:T(4,128)S(1)}, f32[1,4]{0,1:T(4,128)S(1)}, f32[1,4]{0,1:T(4,128)S(1)}, f32[1,4]{0,1:T(4,12...) fusion(f32[1,4]{0,1:T(4,128)S(1)} %get-tuple-element.27, ...), kind=kLoop, calls=%fused_computation.824 | loop fusion | flops 416 | bytes 532 | tf_op jit(solution)/shard_map/div | solution.py:46
  399.8 26.2 %subtract_divide_fusion.6 = f32[1,4]{0,1:T(4,128)S(1)} fusion(f32[1,4]{0,1:T(4,128)S(1)} %get-tuple-element.19, f32[1,4]{0,1:T(4,128)S(1)} %get-tuple-element.18, f32[1,4]{0,1:T(4,128)S(1)} %get-tuple-element.17, f32[1,4]{0,1:T(4,128)S(1)} %get-tuple-element.16, f32[1,4]{0,1:T(4,128)S(1)} %get-tuple-element.15, f32[1,4]{0,1:T(4,128)S(1)} %get-tuple-element.14, ...), kind=kLoop, calls=%fused_computation.821 | loop fusion | flops 324 | bytes 376 | tf_op jit(solution)/shard_map/div | solution.py:46
  426.1 18.9 %subtract_divide_fusion.7 = f32[1,4]{0,1:T(4,128)S(1)} fusion(f32[1,4]{0,1:T(4,128)S(1)} %get-tuple-element.19, f32[1,4]{0,1:T(4,128)S(1)} %get-tuple-element.18, f32[1,4]{0,1:T(4,128)S(1)} %get-tuple-element.17, f32[1,4]{0,1:T(4,128)S(1)} %get-tuple-element.16, f32[1,4]{0,1:T(4,128)S(1)} %get-tuple-element.15, f32[1,4]{0,1:T(4,128)S(1)} %get-tuple-element.14, ...), kind=kLoop, calls=%fused_computation.822 | loop fusion | flops 228 | bytes 312 | tf_op jit(solution)/shard_map/div | solution.py:46
  444.9 12.0 %subtract_divide_fusion.8 = f32[1,4]{0,1:T(4,128)S(1)} fusion(f32[1,4]{0,1:T(4,128)S(1)} %get-tuple-element.19, f32[1,4]{0,1:T(4,128)S(1)} %get-tuple-element.18, f32[1,4]{0,1:T(4,128)S(1)} %get-tuple-element.17, f32[1,4]{0,1:T(4,128)S(1)} %get-tuple-element.16, f32[1,4]{0,1:T(4,128)S(1)} %get-tuple-element.15, f32[1,4]{0,1:T(4,128)S(1)} %get-tuple-element.14, ...), kind=kLoop, calls=%fused_computation.823 | loop fusion | flops 144 | bytes 252 | tf_op jit(solution)/shard_map/div | solution.py:46
  457.3 2.3 collective-permute-start.19
  459.8 2.4 collective-permute-done.19
  462.2 1.9 collective-permute-done.18
  465.8 1.8 collective-permute-done.20
  467.9 1.7 collective-permute-start.23
  470.0 11.6 %collective-permute-done.23 = f32[4,5,3,10,1]{4,3,2,1,0:T(8,128)S(1)} collective-permute-done((f32[4,5,3,10,1]{4,3,2,1,0:T(8,128)S(1)}, f32[4,5,3,10,1]{4,3,2,1,0:T(8,128)S(1)}, u32[]{:S(2)}, u32[]{:S(2)}) %collective-permute-start.23) | collective-permute-done | bytes 2432 | tf_op jit(solution)/shard_map/ppermute | solution.py:18
  481.5 9.8 %collective-permute-done.22 = f32[4,5,3,10,1]{4,3,2,1,0:T(8,128)S(1)} collective-permute-done((f32[4,5,3,10,1]{4,3,2,1,0:T(8,128)S(1)}, f32[4,5,3,10,1]{4,3,2,1,0:T(8,128)S(1)}, u32[]{:S(2)}, u32[]{:S(2)}) %collective-permute-start.22) | collective-permute-done | bytes 2432 | tf_op jit(solution)/shard_map/ppermute | solution.py:16
  493.4 2.8 bitcast_subtract_fusion
  (160 shorter events, 37.1 us)
Async XLA Ops:
  0.6 59.1 %copy-start = (bf16[27,5,5,1,8,128]{5,4,3,2,1,0:T(8,128)(2,1)S(1)}, bf16[27,5,5,1,8,128]{5,4,3,2,1,0:T(8,128)(2,1)}, u32[]{:S(2)}) copy-start(bf16[27,5,5,1,8,128]{5,4,3,2,1,0:T(8,128)(2,1)} %param.4) | copy-start | bytes 4147204
  56.3 9.8 %collective-permute-start.1 = (f32[4,5,1,8,128]{4,3,2,1,0:T(8,128)S(1)}, f32[4,5,1,8,128]{4,3,2,1,0:T(8,128)S(1)}, u32[]{:S(2)}, u32[]{:S(2)}) collective-permute-start(f32[4,5,1,8,128]{4,3,2,1,0:T(8,128)S(1)} %pad_maximum_fusion.5), channel_id=1, source_target_pairs={{16,0},{0,16},{17,1},{1,17},{18,2},{2,18},{19,3},{3,19},{20,4},{4,... | collective-permute-start | bytes 245768 | tf_op jit(solution)/shard_map/ppermute | solution.py:18
  58.7 7.5 %collective-permute-start = (f32[4,5,1,8,128]{4,3,2,1,0:T(8,128)S(1)}, f32[4,5,1,8,128]{4,3,2,1,0:T(8,128)S(1)}, u32[]{:S(2)}, u32[]{:S(2)}) collective-permute-start(f32[4,5,1,8,128]{4,3,2,1,0:T(8,128)S(1)} %pad_maximum_fusion.5), channel_id=1, source_target_pairs={{0,16},{16,0},{1,17},{17,1},{2,18},{18,2},{3,19},{19,3},{4,20},{20... | collective-permute-start | bytes 245768 | tf_op jit(solution)/shard_map/ppermute | solution.py:16
  66.2 1.6 collective-permute-start.3
  66.2 3.8 collective-permute-start.2
  70.3 13.9 %collective-permute-start.5 = (f32[4,5,3,10,1]{4,3,2,1,0:T(8,128)S(1)}, f32[4,5,3,10,1]{4,3,2,1,0:T(8,128)S(1)}, u32[]{:S(2)}, u32[]{:S(2)}) collective-permute-start(f32[4,5,3,10,1]{4,3,2,1,0:T(8,128)S(1)} %get-tuple-element.618), channel_id=1, source_target_pairs={{1,0},{2,1},{3,2},{0,3},{5,4},{6,5},{7,6},{4,7},{9,8},{10,9},{11,1... | collective-permute-start | bytes 7208 | tf_op jit(solution)/shard_map/ppermute | solution.py:18
  72.5 23.3 %collective-permute-start.4 = (f32[4,5,3,10,1]{4,3,2,1,0:T(8,128)S(1)}, f32[4,5,3,10,1]{4,3,2,1,0:T(8,128)S(1)}, u32[]{:S(2)}, u32[]{:S(2)}) collective-permute-start(f32[4,5,3,10,1]{4,3,2,1,0:T(8,128)S(1)} %get-tuple-element.617), channel_id=1, source_target_pairs={{0,1},{1,2},{2,3},{3,0},{4,5},{5,6},{6,7},{7,4},{8,9},{9,10},{10,1... | collective-permute-start | bytes 7208 | tf_op jit(solution)/shard_map/ppermute | solution.py:16
  138.9 9.5 %copy-start.4 = (f32[4,4]{1,0:T(4,128)}, f32[4,4]{1,0:T(4,128)S(1)}, u32[]{:S(2)}) copy-start(f32[4,4]{1,0:T(4,128)S(1)} %get-tuple-element.9) | copy-start | bytes 196
  148.5 4.8 collective-permute-start.7
  150.8 4.4 collective-permute-start.6
  155.3 1.6 collective-permute-start.9
  155.4 3.4 collective-permute-start.8
  160.0 13.8 %collective-permute-start.11 = (f32[4,5,3,10,1]{4,3,2,1,0:T(8,128)}, f32[4,5,3,10,1]{4,3,2,1,0:T(8,128)}, u32[]{:S(2)}, u32[]{:S(2)}) collective-permute-start(f32[4,5,3,10,1]{4,3,2,1,0:T(8,128)} %get-tuple-element.616), channel_id=1, source_target_pairs={{1,0},{2,1},{3,2},{0,3},{5,4},{6,5},{7,6},{4,7},{9,8},{10,9},{11,1... | collective-permute-start | bytes 7208 | tf_op jit(solution)/shard_map/ppermute | solution.py:18
  161.9 22.5 %collective-permute-start.10 = (f32[4,5,3,10,1]{4,3,2,1,0:T(8,128)}, f32[4,5,3,10,1]{4,3,2,1,0:T(8,128)}, u32[]{:S(2)}, u32[]{:S(2)}) collective-permute-start(f32[4,5,3,10,1]{4,3,2,1,0:T(8,128)} %get-tuple-element.615), channel_id=1, source_target_pairs={{0,1},{1,2},{2,3},{3,0},{4,5},{5,6},{6,7},{7,4},{8,9},{9,10},{10,1... | collective-permute-start | bytes 7208 | tf_op jit(solution)/shard_map/ppermute | solution.py:16
  237.9 5.1 %collective-permute-start.13 = (f32[4,5,1,8,128]{4,3,2,1,0:T(8,128)S(1)}, f32[4,5,1,8,128]{4,3,2,1,0:T(8,128)S(1)}, u32[]{:S(2)}, u32[]{:S(2)}) collective-permute-start(f32[4,5,1,8,128]{4,3,2,1,0:T(8,128)S(1)} %pad_maximum_fusion.7), channel_id=1, source_target_pairs={{16,0},{0,16},{17,1},{1,17},{18,2},{2,18},{19,3},{3,19},{20,4},{4,... | collective-permute-start | bytes 245768 | tf_op jit(solution)/shard_map/ppermute | solution.py:18
  240.3 4.4 collective-permute-start.12
  244.8 1.6 collective-permute-start.15
  244.8 3.4 collective-permute-start.14
  248.2 3.5 copy-start.3
  249.4 14.2 %collective-permute-start.17 = (f32[4,5,3,10,1]{4,3,2,1,0:T(8,128)}, f32[4,5,3,10,1]{4,3,2,1,0:T(8,128)}, u32[]{:S(2)}, u32[]{:S(2)}) collective-permute-start(f32[4,5,3,10,1]{4,3,2,1,0:T(8,128)} %get-tuple-element.614), channel_id=1, source_target_pairs={{1,0},{2,1},{3,2},{0,3},{5,4},{6,5},{7,6},{4,7},{9,8},{10,9},{11,1... | collective-permute-start | bytes 7208 | tf_op jit(solution)/shard_map/ppermute | solution.py:18
  251.7 22.2 %collective-permute-start.16 = (f32[4,5,3,10,1]{4,3,2,1,0:T(8,128)}, f32[4,5,3,10,1]{4,3,2,1,0:T(8,128)}, u32[]{:S(2)}, u32[]{:S(2)}) collective-permute-start(f32[4,5,3,10,1]{4,3,2,1,0:T(8,128)} %get-tuple-element.613), channel_id=1, source_target_pairs={{0,1},{1,2},{2,3},{3,0},{4,5},{5,6},{6,7},{7,4},{8,9},{9,10},{10,1... | collective-permute-start | bytes 7208 | tf_op jit(solution)/shard_map/ppermute | solution.py:16
  276.8 3.0 copy-start.5
  457.3 34.0 %copy-start.1 = (f32[1,4,40,128]{3,2,1,0:T(8,128)}, f32[1,4,40,128]{3,2,1,0:T(8,128)S(1)}, u32[]{:S(2)}) copy-start(f32[1,4,40,128]{3,2,1,0:T(8,128)S(1)} %copy.75) | copy-start | bytes 245764
  457.3 4.9 collective-permute-start.19
  459.7 4.4 collective-permute-start.18
  464.2 1.6 collective-permute-start.21
  464.2 3.4 collective-permute-start.20
  467.9 13.6 %collective-permute-start.23 = (f32[4,5,3,10,1]{4,3,2,1,0:T(8,128)S(1)}, f32[4,5,3,10,1]{4,3,2,1,0:T(8,128)S(1)}, u32[]{:S(2)}, u32[]{:S(2)}) collective-permute-start(f32[4,5,3,10,1]{4,3,2,1,0:T(8,128)S(1)} %get-tuple-element.612), channel_id=1, source_target_pairs={{1,0},{2,1},{3,2},{0,3},{5,4},{6,5},{7,6},{4,7},{9,8},{10,9},{11,1... | collective-permute-start | bytes 7208 | tf_op jit(solution)/shard_map/ppermute | solution.py:18
  469.6 21.7 %collective-permute-start.22 = (f32[4,5,3,10,1]{4,3,2,1,0:T(8,128)S(1)}, f32[4,5,3,10,1]{4,3,2,1,0:T(8,128)S(1)}, u32[]{:S(2)}, u32[]{:S(2)}) collective-permute-start(f32[4,5,3,10,1]{4,3,2,1,0:T(8,128)S(1)} %get-tuple-element.611), channel_id=1, source_target_pairs={{0,1},{1,2},{2,3},{3,0},{4,5},{5,6},{6,7},{7,4},{8,9},{9,10},{10,1... | collective-permute-start | bytes 7208 | tf_op jit(solution)/shard_map/ppermute | solution.py:16
  492.5 0.9 copy-start.2
where the time goes:
time: 499 us; the launch traced here: 496 us
  other arithmetic  182 us (36%)
  blocking collectives  158 us (32%)
  waiting for transfers between devices  114 us (23%)
  starting transfers between devices  20.5 us (4%)
  local copies, waits for them, and re-layouts  13.8 us (3%)
  matrix products  6.05 us (1%)
    psum x3, blocking collectives, shards(): lax.psum((dot_high(stacked, workspace.T), dot_high(workspace, workspace.T...  116 us
    div x4, other arithmetic, upper_solve(): solved[row_pos] = accum / factor[row_pos, row_pos]  87.1 us
    div x6, other arithmetic, lower_solve(): solved.append(accum / factor[row_pos, row_pos])  69.5 us
    ppermute x12, waiting for transfers between devices, extended(): lax.ppermute(head, axis, [((i + 1) % count, i) for i in range(count)])  58 us
    ppermute x12, waiting for transfers between devices, extended(): lax.ppermute(tail, axis, [(i, (i + 1) % count) for i in range(count)])  55.6 us
    psum x1, blocking collectives, shards(): start_matrix = lax.psum(dot_high(flat_rhs, flat_rhs.T), ('gx', 'gy', 'gz'))  41.9 us
    ppermute x12, starting transfers between devices, extended(): lax.ppermute(head, axis, [((i + 1) % count, i) for i in range(count)])  17.7 us
  transfers between devices with their start and end apart: 24, of which 22 were waited for; matrix products, arithmetic and copies ran while one was open for 2% of the time, Pallas kernels for 0%

commit v1 on v0

v1 whole, which is shorter than its diff:
```python
import functools
import itertools

import jax
import jax.numpy as jnp
from jax import lax
from jax.experimental import pallas as pl
from jax.experimental.pallas import tpu as pltpu
from jax.sharding import PartitionSpec as P

ITERS = 3
SHIFT = 9.0
MESH = pl.DeviceIdType.MESH
AXES = ("gx", "gy", "gz")


def make_kernel(sizes, rhs, comp, rows, lanes):
    count_x, count_y, count_z = sizes
    devices = count_x * count_y * count_z
    fields = rhs * comp
    merged = count_x == 2
    plane_steps = (0, 1) if merged else (0, 1, -1)
    planes = len(plane_steps)
    pair_list = []
    vectors = rhs * (ITERS + 1)
    for step in range(1, ITERS + 1):
        for mine in range(rhs * step, rhs * (step + 1)):
            for other in range(0, mine + 1):
                pair_list.append((mine, other))
    pair_slot = {pair: slot for slot, pair in enumerate(pair_list)}
    pair_pad = -(-len(pair_list) // 128) * 128

    def kernel(
        right_ref, jac_hbm, sol_ref, res_ref,
        basis, prods, jac_low, jac, shifted, packs, edge_rows, edge_corner,
        far_plane, halo_rows, halo_cols, halo_corner, tops, gram, part, parts,
        jac_sem, send_sem, recv_sem, red_send, red_recv,
    ):
        my_x, my_y, my_z = (lax.axis_index(axis) for axis in AXES)
        me = (my_x * count_y + my_y) * count_z + my_z

        def coords(index):
            return (index // (count_y * count_z), index // count_z % count_y, index % count_z)

        loads = pltpu.make_async_copy(jac_hbm, jac_low, jac_sem)
        loads.start()

        barrier = pltpu.get_barrier_semaphore()

        def greet(step, carry):
            pl.semaphore_signal(
                barrier, inc=1, device_id=coords(lax.rem(me + step, devices)), device_id_type=MESH
            )
            return carry

        lax.fori_loop(1, devices, greet, 0)

        lane = lax.broadcasted_iota(jnp.int32, (rows, lanes), 1)
        sub = lax.broadcasted_iota(jnp.int32, (rows, lanes), 0)

        def field(turn, at):
            return right_ref[at] if turn == 0 else basis[turn - 1, at]

        def pack(turn):
            packed = jnp.zeros((rows, lanes), jnp.float32)
            for at in range(fields):
                value = field(turn, at)
                edge_rows[turn, 0, at : at + 1, :] = value[rows - 1 : rows]
                edge_rows[turn, 1, at : at + 1, :] = value[0:1]
                packed = jnp.where(lane // 2 == at, pltpu.roll(value, 2 * at + 1, 1), packed)
            packs[turn] = packed
            edge_corner[turn, 0] = packed[rows - 1 : rows]
            edge_corner[turn, 1] = packed[0:1]

        def messages(turn):
            found = []
            for plane, step_x in enumerate(plane_steps):
                for dy, dz in itertools.product((0, 1, -1), (0, 1, -1)):
                    side_y = 0 if dy == 1 else 1
                    side_z = 0 if dz == 1 else 1
                    if dy == 0 and dz == 0:
                        if plane == 0:
                            continue
                        source = right_ref if turn == 0 else basis.at[turn - 1]
                        target = far_plane.at[turn, plane - 1]
                    elif dz == 0:
                        source = edge_rows.at[turn, side_y]
                        target = halo_rows.at[turn, plane, side_y]
                    elif dy == 0:
                        source = packs.at[turn]
                        target = halo_cols.at[turn, plane, side_z]
                    else:
                        source = edge_corner.at[turn, side_y]
                        target = halo_corner.at[turn, plane, side_y, side_z]
                    slot = plane * 9 + (dy + 1) * 3 + dz + 1
                    copy = pltpu.make_async_remote_copy(
                        src_ref=source,
                        dst_ref=target,
                        send_sem=send_sem.at[turn, slot],
                        recv_sem=recv_sem.at[turn, slot],
                        device_id=(
                            lax.rem(my_x + step_x + count_x, count_x),
                            lax.rem(my_y + dy + count_y, count_y),
                            jnp.clip(my_z + dz, 0, count_z - 1),
                        ),
                        device_id_type=MESH,
                    )
                    found.append((plane, dz, copy))
            return found

        above = my_z < count_z - 1
        below = my_z > 0

        def for_each(copies, act, sending):
            for step_z in (1, -1, 0):
                chosen = [copy for _, dz, copy in copies if dz == step_z]
                if step_z == 0:
                    for copy in chosen:
                        act(copy)
                else:
                    present = above if (step_z == 1) == sending else below

                    @pl.when(present)
                    def _():
                        for copy in chosen:
                            act(copy)

        def shift_plane(turn, plane):
            low = jnp.where(below, pltpu.roll(halo_cols[turn, plane, 0], 1, 1), 0.0)
            high = jnp.where(above, pltpu.roll(halo_cols[turn, plane, 1], lanes - 1, 1), 0.0)
            mixed = jnp.where(lane % 2 == 1, low, high)
            wide_lane = lax.broadcasted_iota(jnp.int32, (fields, lanes), 1)
            wide_at = lax.broadcasted_iota(jnp.int32, (fields, lanes), 0)
            for side in range(2):
                strip = halo_rows[turn, plane, side]
                low_row = jnp.where(below, halo_corner[turn, plane, side, 0], 0.0)
                high_row = jnp.where(above, halo_corner[turn, plane, side, 1], 0.0)
                low_col = jnp.sum(
                    jnp.where(wide_lane == 2 * wide_at, low_row, 0.0), axis=1, keepdims=True
                )
                high_col = jnp.sum(
                    jnp.where(wide_lane == 2 * wide_at + 1, high_row, 0.0), axis=1, keepdims=True
                )
                tops[side, 0] = jnp.where(wide_lane == 0, low_col, pltpu.roll(strip, 1, 1))
                tops[side, 1] = strip
                tops[side, 2] = jnp.where(
                    wide_lane == lanes - 1, high_col, pltpu.roll(strip, lanes - 1, 1)
                )
            for at in range(fields):
                value = field(turn, at) if plane == 0 else far_plane[turn, plane - 1, at]
                edge = pltpu.roll(mixed, lanes - 2 * at - 1, 1)
                along = (
                    jnp.where(lane == 0, edge, pltpu.roll(value, 1, 1)),
                    value,
                    jnp.where(lane == lanes - 1, edge, pltpu.roll(value, lanes - 1, 1)),
                )
                for dz in range(3):
                    shifted[dz, at] = jnp.where(
                        sub == 0, tops[0, dz, at : at + 1, :], pltpu.roll(along[dz], 1, 0)
                    )
                    shifted[3 + dz, at] = along[dz]
                    shifted[6 + dz, at] = jnp.where(
                        sub == rows - 1,
                        tops[1, dz, at : at + 1, :],
                        pltpu.roll(along[dz], rows - 1, 0),
                    )

        def stencil(plane, totals):
            def body(near, sums):
                sums = list(sums)
                for source in range(comp):
                    blocks = [jac[plane, near, a * comp + source] for a in range(comp)]
                    for r in range(rhs):
                        value = shifted[near, r * comp + source]
                        for a in range(comp):
                            sums[r * comp + a] = sums[r * comp + a] + blocks[a] * value
                return tuple(sums)

            return lax.fori_loop(0, 9, body, totals)

        def vector(index, c):
            if index < rhs:
                return right_ref[index * comp + c]
            return prods[index // rhs - 1, (index % rhs) * comp + c]

        def dots(step):
            for mine in range(rhs * step, rhs * (step + 1)):
                own = [vector(mine, c) for c in range(comp)]
                for other in range(0, mine + 1):
                    total = own[0] * vector(other, 0)
                    for c in range(1, comp):
                        total = total + own[c] * vector(other, c)
                    gram[pair_slot[mine, other]] = total

        for slot in range(len(pair_list), pair_pad):
            gram[slot] = jnp.zeros((rows, lanes), jnp.float32)
        pack(0)
        pl.semaphore_wait(barrier, devices - 1)

        for turn in range(ITERS):
            copies = messages(turn)
            for_each(copies, lambda copy: copy.start(), True)
            if turn == 0:
                loads.wait()

                def widen(near, carry):
                    for entry in range(comp * comp):
                        jac[0, near, entry] = jac_low[9 + near, entry].astype(jnp.float32)
                        first = jac_low[near, entry].astype(jnp.float32)
                        last = jac_low[18 + near, entry].astype(jnp.float32)
                        if merged:
                            jac[1, near, entry] = first + last
                        else:
                            jac[1, near, entry] = first
                            jac[2, near, entry] = last
                    return carry

                lax.fori_loop(0, 9, widen, 0)
            else:
                dots(turn)
            totals = tuple(jnp.zeros((rows, lanes), jnp.float32) for _ in range(fields))
            for plane in range(planes):
                mine = [copy for copy in copies if copy[0] == plane]
                for_each(mine, lambda copy: copy.wait_recv(), False)
                shift_plane(turn, plane)
                totals = stencil(plane, totals)
            for at in range(fields):
                prods[turn, at] = totals[at]
                if turn < ITERS - 1:
                    basis[turn, at] = totals[at] - SHIFT * field(turn, at)
            if turn < ITERS - 1:
                pack(turn + 1)

        dots(ITERS)
        sums = jnp.sum(gram[...], axis=1)
        row = lax.dot_general(
            jnp.ones((rows, lanes), jnp.float32),
            sums,
            (((1,), (1,)), ((), ())),
            precision=lax.Precision.HIGHEST,
            preferred_element_type=jnp.float32,
        )
        part[...] = row[0:1]

        def spread(step):
            return pltpu.make_async_remote_copy(
                src_ref=part,
                dst_ref=parts.at[me],
                send_sem=red_send.at[step],
                recv_sem=red_recv.at[step],
                device_id=coords(lax.rem(me + step, devices)),
                device_id_type=MESH,
            )

        def gathered(step):
            return pltpu.make_async_remote_copy(
                src_ref=part,
                dst_ref=parts.at[lax.rem(me + devices - step, devices)],
                send_sem=red_send.at[step],
                recv_sem=red_recv.at[step],
                device_id=coords(lax.rem(me + step, devices)),
                device_id_type=MESH,
            )

        def begin(step, carry):
            spread(step).start()
            return carry

        def finish(step, carry):
            gathered(step).wait_recv()
            return carry

        lax.fori_loop(1, devices, begin, 0)
        parts[me] = part[...]
        lax.fori_loop(1, devices, finish, 0)
        total_row = jnp.broadcast_to(jnp.sum(parts[...], axis=0), (rows, pair_pad))

        def entry(mine, other):
            slot = pair_slot[max(mine, other), min(mine, other)]
            return jnp.broadcast_to(total_row[:, slot : slot + 1], (rows, lanes))

        size = rhs * ITERS
        matrix = {}
        target = {}
        for i in range(size):
            for j in range(i + 1):
                matrix[i, j] = entry(rhs + i, rhs + j)
            for r in range(rhs):
                target[i, r] = entry(rhs + i, r)
        inverse = {}
        for k in range(size):
            inverse[k] = 1.0 / matrix[k, k]
            for i in range(k + 1, size):
                ratio = matrix[i, k] * inverse[k]
                for j in range(k + 1, i + 1):
                    matrix[i, j] = matrix[i, j] - ratio * matrix[j, k]
                for r in range(rhs):
                    target[i, r] = target[i, r] - ratio * target[k, r]
        weights = {}
        for k in range(size - 1, -1, -1):
            for r in range(rhs):
                accum = target[k, r]
                for later in range(k + 1, size):
                    accum = accum - matrix[later, k] * weights[later, r]
                weights[k, r] = accum * inverse[k]
        for r in range(rhs):
            for c in range(comp):
                found = jnp.zeros((rows, lanes), jnp.float32)
                left = right_ref[r * comp + c]
                for j in range(size):
                    found = found + weights[j, r] * field(j // rhs, (j % rhs) * comp + c)
                    left = left - weights[j, r] * prods[j // rhs, (j % rhs) * comp + c]
                sol_ref[r * comp + c] = found
                res_ref[r * comp + c] = left

        for turn in range(ITERS):
            for_each(messages(turn), lambda copy: copy.wait_send(), True)

        def settle(step, carry):
            spread(step).wait_send()
            return carry

        lax.fori_loop(1, devices, settle, 0)

    full = (rows, lanes)
    scratch = [
        pltpu.VMEM((ITERS - 1, fields) + full, jnp.float32),
        pltpu.VMEM((ITERS, fields) + full, jnp.float32),
        pltpu.VMEM((27, comp * comp) + full, jnp.bfloat16),
        pltpu.VMEM((planes, 9, comp * comp) + full, jnp.float32),
        pltpu.VMEM((9, fields) + full, jnp.float32),
        pltpu.VMEM((ITERS,) + full, jnp.float32),
        pltpu.VMEM((ITERS, 2, fields, lanes), jnp.float32),
        pltpu.VMEM((ITERS, 2, 1, lanes), jnp.float32),
        pltpu.VMEM((ITERS, planes - 1, fields) + full, jnp.float32),
        pltpu.VMEM((ITERS, planes, 2, fields, lanes), jnp.float32),
        pltpu.VMEM((ITERS, planes, 2) + full, jnp.float32),
        pltpu.VMEM((ITERS, planes, 2, 2, 1, lanes), jnp.float32),
        pltpu.VMEM((2, 3, fields, lanes), jnp.float32),
        pltpu.VMEM((pair_pad,) + full, jnp.float32),
        pltpu.VMEM((1, pair_pad), jnp.float32),
        pltpu.VMEM((devices, 1, pair_pad), jnp.float32),
        pltpu.SemaphoreType.DMA,
        pltpu.SemaphoreType.DMA((ITERS, planes * 9)),
        pltpu.SemaphoreType.DMA((ITERS, planes * 9)),
        pltpu.SemaphoreType.DMA((devices,)),
        pltpu.SemaphoreType.DMA((devices,)),
    ]
    return kernel, scratch


def shards(sizes, right_side, jacobian):
    rhs, comp, extent_x, rows, lanes = right_side.shape
    assert extent_x == 1
    kernel, scratch = make_kernel(sizes, rhs, comp, rows, lanes)
    shape = jax.ShapeDtypeStruct((rhs * comp, rows, lanes), jnp.float32)
    vmem = pl.BlockSpec(memory_space=pltpu.VMEM)
    found, left = pl.pallas_call(
        kernel,
        out_shape=(shape, shape),
        in_specs=[vmem, pl.BlockSpec(memory_space=pl.ANY)],
        out_specs=(vmem, vmem),
        scratch_shapes=scratch,
        compiler_params=pltpu.CompilerParams(collective_id=0, has_side_effects=True),
    )(
        right_side.reshape(rhs * comp, rows, lanes),
        jacobian.reshape(27, comp * comp, rows, lanes),
    )
    return found.reshape(right_side.shape), left.reshape(right_side.shape)


def solution(mesh):
    sizes = tuple(mesh.shape[axis] for axis in AXES)
    in_specs = (P(None, None, *AXES), P(None, None, None, *AXES))
    out_specs = (P(None, None, *AXES), P(None, None, *AXES))
    return jax.shard_map(
        functools.partial(shards, sizes), mesh=mesh, in_specs=in_specs, out_specs=out_specs, check_vma=False
    )
```

time: 499 us -> 33.5 us (0.07)
  other arithmetic: 182 us -> 0 us
  blocking collectives: 158 us -> 0 us
  waiting for transfers between devices: 114 us -> 0 us
  Pallas kernels: 0 us -> 29.6 us
  starting transfers between devices: 20.5 us -> 0 us
  local copies, waits for them, and re-layouts: 13.8 us -> 3.05 us
  matrix products: 6.05 us -> 0 us
    psum x4 -> x0, blocking collectives: 158 us -> none  [the longest x3 116 us: shards(): lax.psum((dot_high(stacked, workspace.T), dot_high(workspace, workspace.T...]
    div x15 -> x0, other arithmetic: 157 us -> none  [the longest x4 87.1 us: upper_solve(): solved[row_pos] = accum / factor[row_pos, row_pos]]
    ppermute x24 -> x0, waiting for transfers between devices: 114 us -> none  [the longest x12 58 us: extended(): lax.ppermute(head, axis, [((i + 1) % count, i) for i in range(count)])]
    pallas_call x0 -> x1, Pallas kernels: none -> 29.6 us  [shards(): pl.pallas_call(kernel, out_shape=(shape, shape), in_specs=[vmem, pl.Block...]
    ppermute x24 -> x0, starting transfers between devices: 20.5 us -> none  [the longest x12 17.7 us: extended(): lax.ppermute(head, axis, [((i + 1) % count, i) for i in range(count)])]
    slice x12 -> x0, local copies, waits for them, and re-layouts: 8.19 us -> none  [the longest x4 2.61 us: extended(): lax.slice_in_dim(cells, cells.shape[dim] - width, cells.shape[dim], axis=...]
    add x3 -> x0, other arithmetic: 6.08 us -> none  [apply_operator(): total = total + block[None, :, source_comp] * piece[:, source_comp][:, None]]
    dot_general x15 -> x0, matrix products: 6.05 us -> none  [dot_high(): jnp.dot(left, right, precision=lax.Precision.HIGHEST, preferred_element_t...]
  transfers between devices with their start and end apart: 24 -> 0, of which waited for: 22 -> 0; matrix products, arithmetic and copies ran while one was open for 2% -> 0% of each run, Pallas kernels for 0% -> 0%
where the time goes in v1:
time: 33.5 us; the launch traced here: 33.3 us
  Pallas kernels  29.6 us (88%)
  local copies, waits for them, and re-layouts  3.05 us (9%)
  between operations  0.64 us (2%)
    pallas_call x1, Pallas kernels, shards(): pl.pallas_call(kernel, out_shape=(shape, shape), in_specs=[vmem, pl.Block...  29.6 us
    unnamed x2, local copies, waits for them, and re-layouts  3.05 us

profile of v1, /device:TPU:0, one launch (start us, length us, event | category | flops | bytes accessed | tf_op | source)
XLA Modules:
  0.0 33.3 jit_solution(12569435572100437360)
XLA Ops:
  0.6 29.6 %shard_map.41 = (f32[20,8,128]{2,1,0:T(8,128)}, f32[20,8,128]{2,1,0:T(8,128)}) custom-call(f32[20,8,128]{2,1,0:T(8,128)} %bitcast.9, bf16[27,25,8,128]{3,2,1,0:T(8,128)(2,1)} %bitcast.8), custom_call_target="tpu_custom_call" | custom-call | tf_op jit(solution)/shard_map/pallas_call | solution.py:358
  30.2 1.5 %copy.8 = f32[4,5,1,8,128]{4,3,2,1,0:T(8,128)} copy(f32[4,5,1,8,128]{4,3,2,1,0:T(8,128)} %bitcast.11) | data formatting | bytes 163840
  31.8 1.5 %copy.9 = f32[4,5,1,8,128]{4,3,2,1,0:T(8,128)} copy(f32[4,5,1,8,128]{4,3,2,1,0:T(8,128)} %bitcast.10) | data formatting | bytes 163840

commit v2 on v1

--- a/solution.py
+++ b/solution.py
@@ -21,6 +21,7 @@
     merged = count_x == 2
     plane_steps = (0, 1) if merged else (0, 1, -1)
     planes = len(plane_steps)
+    slots = 9 + rhs
     pair_list = []
     vectors = rhs * (ITERS + 1)
     for step in range(1, ITERS + 1):
@@ -75,37 +76,42 @@
         def messages(turn):
             found = []
             for plane, step_x in enumerate(plane_steps):
-                for dy, dz in itertools.product((0, 1, -1), (0, 1, -1)):
+                for dy, dz in itertools.product((1, -1, 0), (1, -1, 0)):
                     side_y = 0 if dy == 1 else 1
                     side_z = 0 if dz == 1 else 1
                     if dy == 0 and dz == 0:
                         if plane == 0:
                             continue
-                        source = right_ref if turn == 0 else basis.at[turn - 1]
-                        target = far_plane.at[turn, plane - 1]
+                        values = right_ref if turn == 0 else basis.at[turn - 1]
+                        moves = [
+                            (values.at[pl.ds(r * comp, comp)], far_plane.at[turn, plane - 1, pl.ds(r * comp, comp)])
+                            for r in range(rhs)
+                        ]
                     elif dz == 0:
-                        source = edge_rows.at[turn, side_y]
-                        target = halo_rows.at[turn, plane, side_y]
+                        moves = [(edge_rows.at[turn, side_y], halo_rows.at[turn, plane, side_y])]
                     elif dy == 0:
-                        source = packs.at[turn]
-                        target = halo_cols.at[turn, plane, side_z]
+                        moves = [(packs.at[turn], halo_cols.at[turn, plane, side_z])]
                     else:
-                        source = edge_corner.at[turn, side_y]
-                        target = halo_corner.at[turn, plane, side_y, side_z]
-                    slot = plane * 9 + (dy + 1) * 3 + dz + 1
-                    copy = pltpu.make_async_remote_copy(
-                        src_ref=source,
-                        dst_ref=target,
-                        send_sem=send_sem.at[turn, slot],
-                        recv_sem=recv_sem.at[turn, slot],
-                        device_id=(
-                            lax.rem(my_x + step_x + count_x, count_x),
-                            lax.rem(my_y + dy + count_y, count_y),
-                            jnp.clip(my_z + dz, 0, count_z - 1),
-                        ),
-                        device_id_type=MESH,
-                    )
-                    found.append((plane, dz, copy))
+                        moves = [(edge_corner.at[turn, side_y], halo_corner.at[turn, plane, side_y, side_z])]
+                    for part_at, (source, target) in enumerate(moves):
+                        slot = plane * slots
+                        if len(moves) == 1:
+                            slot = slot + (dy + 1) * 3 + dz + 1
+                        else:
+                            slot = slot + 9 + part_at
+                        copy = pltpu.make_async_remote_copy(
+                            src_ref=source,
+                            dst_ref=target,
+                            send_sem=send_sem.at[turn, slot],
+                            recv_sem=recv_sem.at[turn, slot],
+                            device_id=(
+                                lax.rem(my_x + step_x + count_x, count_x),
+                                lax.rem(my_y + dy + count_y, count_y),
+                                jnp.clip(my_z + dz, 0, count_z - 1),
+                            ),
+                            device_id_type=MESH,
+                        )
+                        found.append((plane, dz, copy, part_at if len(moves) > 1 else None))
             return found
 
         above = my_z < count_z - 1
@@ -113,7 +119,7 @@
 
         def for_each(copies, act, sending):
             for step_z in (1, -1, 0):
-                chosen = [copy for _, dz, copy in copies if dz == step_z]
+                chosen = [copy for _, dz, copy, _ in copies if dz == step_z]
                 if step_z == 0:
                     for copy in chosen:
                         act(copy)
@@ -125,7 +131,7 @@
                         for copy in chosen:
                             act(copy)
 
-        def shift_plane(turn, plane):
+        def shift_edges(turn, plane):
             low = jnp.where(below, pltpu.roll(halo_cols[turn, plane, 0], 1, 1), 0.0)
             high = jnp.where(above, pltpu.roll(halo_cols[turn, plane, 1], lanes - 1, 1), 0.0)
             mixed = jnp.where(lane % 2 == 1, low, high)
@@ -146,7 +152,10 @@
                 tops[side, 2] = jnp.where(
                     wide_lane == lanes - 1, high_col, pltpu.roll(strip, lanes - 1, 1)
                 )
-            for at in range(fields):
+            return mixed
+
+        def shift_fields(turn, plane, mixed, first, last):
+            for at in range(first, last):
                 value = field(turn, at) if plane == 0 else far_plane[turn, plane - 1, at]
                 edge = pltpu.roll(mixed, lanes - 2 * at - 1, 1)
                 along = (
@@ -165,18 +174,19 @@
                         pltpu.roll(along[dz], rows - 1, 0),
                     )
 
-        def stencil(plane, totals):
-            def body(near, sums):
+        def stencil(plane, totals, sides):
+            def body(line, sums):
                 sums = list(sums)
-                for source in range(comp):
+                for near, source in itertools.product(range(3), range(comp)):
+                    near = line * 3 + near
                     blocks = [jac[plane, near, a * comp + source] for a in range(comp)]
-                    for r in range(rhs):
+                    for place, r in enumerate(sides):
                         value = shifted[near, r * comp + source]
                         for a in range(comp):
-                            sums[r * comp + a] = sums[r * comp + a] + blocks[a] * value
+                            sums[place * comp + a] = sums[place * comp + a] + blocks[a] * value
                 return tuple(sums)
 
-            return lax.fori_loop(0, 9, body, totals)
+            return list(lax.fori_loop(0, 3, body, tuple(totals)))
 
         def vector(index, c):
             if index < rhs:
@@ -195,39 +205,50 @@
         for slot in range(len(pair_list), pair_pad):
             gram[slot] = jnp.zeros((rows, lanes), jnp.float32)
         pack(0)
+        loads.wait()
+
+        def widen(near, carry):
+            for entry in range(comp * comp):
+                jac[0, near, entry] = jac_low[9 + near, entry].astype(jnp.float32)
+                first = jac_low[near, entry].astype(jnp.float32)
+                last = jac_low[18 + near, entry].astype(jnp.float32)
+                if merged:
+                    jac[1, near, entry] = first + last
+                else:
+                    jac[1, near, entry] = first
+                    jac[2, near, entry] = last
+            return carry
+
+        lax.fori_loop(0, 9, widen, 0)
         pl.semaphore_wait(barrier, devices - 1)
 
         for turn in range(ITERS):
             copies = messages(turn)
             for_each(copies, lambda copy: copy.start(), True)
-            if turn == 0:
-                loads.wait()
-
-                def widen(near, carry):
-                    for entry in range(comp * comp):
-                        jac[0, near, entry] = jac_low[9 + near, entry].astype(jnp.float32)
-                        first = jac_low[near, entry].astype(jnp.float32)
-                        last = jac_low[18 + near, entry].astype(jnp.float32)
-                        if merged:
-                            jac[1, near, entry] = first + last
-                        else:
-                            jac[1, near, entry] = first
-                            jac[2, near, entry] = last
-                    return carry
-
-                lax.fori_loop(0, 9, widen, 0)
-            else:
+            if turn > 0:
                 dots(turn)
-            totals = tuple(jnp.zeros((rows, lanes), jnp.float32) for _ in range(fields))
+            totals = [jnp.zeros((rows, lanes), jnp.float32) for _ in range(fields)]
             for plane in range(planes):
-                mine = [copy for copy in copies if copy[0] == plane]
+                mine = [copy for copy in copies if copy[0] == plane and copy[3] is None]
                 for_each(mine, lambda copy: copy.wait_recv(), False)
-                shift_plane(turn, plane)
-                totals = stencil(plane, totals)
-            for at in range(fields):
-                prods[turn, at] = totals[at]
-                if turn < ITERS - 1:
-                    basis[turn, at] = totals[at] - SHIFT * field(turn, at)
+                mixed = shift_edges(turn, plane)
+                if plane == 0:
+                    shift_fields(turn, plane, mixed, 0, fields)
+                    totals = stencil(plane, totals, range(rhs))
+                    for at in range(fields):
+                        prods[turn, at] = totals[at]
+                    continue
+                for r in range(rhs):
+                    for copy in copies:
+                        if copy[0] == plane and copy[3] == r:
+                            copy[2].wait_recv()
+                    span = range(r * comp, (r + 1) * comp)
+                    shift_fields(turn, plane, mixed, span.start, span.stop)
+                    sums = stencil(plane, [prods[turn, at] for at in span], (r,))
+                    for at, value in zip(span, sums):
+                        prods[turn, at] = value
+                        if turn < ITERS - 1 and plane == planes - 1:
+                            basis[turn, at] = value - SHIFT * field(turn, at)
             if turn < ITERS - 1:
                 pack(turn + 1)
 
@@ -341,12 +362,17 @@
         pltpu.VMEM((1, pair_pad), jnp.float32),
         pltpu.VMEM((devices, 1, pair_pad), jnp.float32),
         pltpu.SemaphoreType.DMA,
-        pltpu.SemaphoreType.DMA((ITERS, planes * 9)),
-        pltpu.SemaphoreType.DMA((ITERS, planes * 9)),
+        pltpu.SemaphoreType.DMA((ITERS, planes * slots)),
+        pltpu.SemaphoreType.DMA((ITERS, planes * slots)),
         pltpu.SemaphoreType.DMA((devices,)),
         pltpu.SemaphoreType.DMA((devices,)),
     ]
     return kernel, scratch
+
+
+def hand_over(found_ref, left_ref, sol_ref, res_ref):
+    sol_ref[...] = found_ref[...]
+    res_ref[...] = left_ref[...]
 
 
 def shards(sizes, right_side, jacobian):
@@ -366,6 +392,12 @@
         right_side.reshape(rhs * comp, rows, lanes),
         jacobian.reshape(27, comp * comp, rows, lanes),
     )
+    found, left = pl.pallas_call(
+        hand_over,
+        out_shape=(shape, shape),
+        in_specs=[vmem, vmem],
+        out_specs=(vmem, vmem),
+    )(found, left)
     return found.reshape(right_side.shape), left.reshape(right_side.shape)
 
 

time: 33.5 us -> 31.3 us (0.934)
  local copies, waits for them, and re-layouts: 3.05 us -> 0 us
  Pallas kernels: 29.6 us -> 30.5 us
    unnamed x2 -> x0, local copies, waits for them, and re-layouts: 3.05 us -> none
    pallas_call x0 -> x1, Pallas kernels: none -> 1.6 us  [shards(): pl.pallas_call(hand_over, out_shape=(shape, shape), in_specs=[vmem, vmem]...]
    pallas_call x1, Pallas kernels: 29.6 us -> 28.9 us  [shards(): pl.pallas_call(kernel, out_shape=(shape, shape), in_specs=[vmem, pl.Block...]
where the time goes in v2:
time: 31.3 us; the launch traced here: 31.1 us
  Pallas kernels  30.5 us (97%)
  between operations  0.64 us (2%)
    pallas_call x1, Pallas kernels, shards(): pl.pallas_call(kernel, out_shape=(shape, shape), in_specs=[vmem, pl.Block...  28.9 us
    pallas_call x1, Pallas kernels, shards(): pl.pallas_call(hand_over, out_shape=(shape, shape), in_specs=[vmem, vmem]...  1.6 us

profile of v2, /device:TPU:0, one launch (start us, length us, event | category | flops | bytes accessed | tf_op | source)
XLA Modules:
  0.0 31.1 jit_solution(2583391599497552359)
XLA Ops:
  0.6 28.9 %shard_map.41 = (f32[20,8,128]{2,1,0:T(8,128)}, f32[20,8,128]{2,1,0:T(8,128)}) custom-call(f32[20,8,128]{2,1,0:T(8,128)} %bitcast.9, bf16[27,25,8,128]{3,2,1,0:T(8,128)(2,1)} %bitcast.8), custom_call_target="tpu_custom_call" | custom-call | tf_op jit(solution)/shard_map/pallas_call | solution.py:384
  29.5 1.6 %shard_map.42 = (f32[20,8,128]{2,1,0:T(8,128)}, f32[20,8,128]{2,1,0:T(8,128)}) custom-call(f32[20,8,128]{2,1,0:T(8,128)} %get-tuple-element.6.found_ref, f32[20,8,128]{2,1,0:T(8,128)} %get-tuple-element.7.left_ref), custom_call_target="tpu_custom_call" | custom-call | tf_op jit(solution)/shard_map/pallas_call | solution.py:395
